TPU v7x, 32 devices: a whole 2x2x4 slice. The times are simulated.
32 devices in a mesh: member: 4 (over y, x), lat: 2 (over core), lon: 4 (over z).
Axes of the slice: x: 2, y: 2, z: 4, core: 2. Of those that a mesh axis runs over, the one named last changes fastest.
Arguments:
- ice_flux: float32 [8, 64, 8, 512], P(('member', 'lat'), 'lon'), parts along dimension 0, may hold values from 0.5 to 1.5
- ice_frac: float32 [8, 64, 512], P(('member', 'lat'), 'lon'), parts along dimension 0, may hold values from 0.05 to 1
- ice_mask: int32 [8, 64, 512], P(('member', 'lat'), 'lon'), parts along dimension 0, may hold values 0 or 1
- ice_area: float32 [8, 64, 512], P(('member', 'lat'), 'lon'), parts along dimension 0, may hold values from 0.7 to 44.3
- route: int32 [8, 64], P(('member', 'lat'), 'lon'), parts along dimension 0, may hold values from 0 to 63, as said below
- ocean_area: float32 [512, 512], P(('member', 'lat'), 'lon'), parts along dimension 0, may hold values from 0.7 to 44.3
- ocean_wet: int32 [512, 512], P(('member', 'lat'), 'lon'), parts along dimension 0, may hold values 0 or 1
- exponent: int32 [8], replicated, may hold values from 0 to 3
Outputs:
- ocean_flux: float32 [8, 512, 512], P(None, ('member', 'lat'), 'lon'), parts along dimension 1
- source_total: float32 [32], P('member'), parts along dimension 0
There are 4 independent parts, one for each index of `member`. A program takes and returns all parts, laid end to end along the dimension named above; an argument that names none is the same for every part. Nothing has to cross between parts.
Inputs may be any that keep to these rules, and one draw needn't show every extreme that they name: Within each latitude tile row, route is a permutation of 0 to 63. The 16 entries of one device name, for every longitude tile k that they name (route // 16 == k), exactly 4 blocks of it.
All inputs are finite; a program needn't handle non-finite values. No bound on the sum of `ice_mask` or of `ocean_wet` on one device may be relied on, other than what follows from the above.
Results may differ from a plain program's by a relative error of at most 0.0003.
Values sent between devices are 32-bit elements; how exact they have to be, the bound alone decides.
A program may use at most 64 MiB of HBM per device.

v0:
```python
import jax
import jax.numpy as jnp
from jax import lax
from jax.sharding import PartitionSpec as P

quantum = 1024.0
limb_base = 65536


def local_units(values, axes):
    return jnp.sum((values * quantum).astype(jnp.int32), axis=axes)


def split_units(total):
    upper_part = total // limb_base
    return (upper_part, total - upper_part * limb_base)


def join_units(upper_part, lower_part):
    return (upper_part.astype(jnp.float32) * limb_base + lower_part.astype(jnp.float32)) / quantum


def body(ice_flux, ice_frac, ice_mask, ice_area, route, ocean_area, ocean_wet, exponent):
    block_count = route.shape[1]
    field_count = ice_flux.shape[2]
    block_cells = ice_flux.shape[3]
    width_cells = ocean_area.shape[1]
    band_rows = block_cells // width_cells
    tile_count = lax.axis_size("lon")
    amount = ice_area * ice_frac * ice_mask.astype(jnp.float32)
    carried = ice_flux * amount[:, :, None, :]
    source_upper, source_lower = split_units(local_units(carried, (0, 1, 3)))
    block_ids = jnp.arange(block_count, dtype=jnp.int32)
    capacity = max(2, block_count // tile_count)
    targets = route[0]
    target_tile = targets // block_count
    block_row = targets % block_count
    earlier = (target_tile[:, None] == target_tile[None, :]) & (
        block_ids[:, None] > block_ids[None, :]
    )
    ordinal = jnp.sum(earlier.astype(jnp.int32), axis=1)
    slot_index = target_tile * capacity + ordinal
    slot_ids = jnp.arange(tile_count * capacity, dtype=jnp.int32)
    selector = (slot_index[None, :] == slot_ids[:, None]).astype(jnp.float32)
    outgoing = jnp.einsum("qs,sfc->qfc", selector, carried[0], precision=lax.Precision.HIGHEST)
    outgoing_rows = (
        jnp.dot(selector, (block_row + 1).astype(jnp.float32), precision=lax.Precision.HIGHEST)
        - 1.0
    )
    received_rows, arrived_rows = (
        lax.all_to_all(outgoing, "lon", split_axis=0, concat_axis=0, tiled=True),
        lax.all_to_all(outgoing_rows, "lon", split_axis=0, concat_axis=0, tiled=True),
    )
    position_mapper = (arrived_rows[None, :] == block_ids.astype(jnp.float32)[:, None]).astype(
        jnp.float32
    )
    block_groups = jnp.einsum(
        "nw,whl->nhl", position_mapper, received_rows, precision=lax.Precision.HIGHEST
    )
    mapped = block_groups.reshape(block_count, field_count, band_rows, width_cells).transpose(
        1, 0, 2, 3
    )
    mapped = mapped.reshape(field_count, block_count * band_rows, width_cells)
    wet_cover = ocean_wet.astype(jnp.float32)
    target_upper, target_lower = split_units(local_units(wet_cover * mapped, (1, 2)))
    wet_upper, wet_lower = split_units(local_units(ocean_area * wet_cover, (0, 1)))
    source_upper, source_lower, target_upper, target_lower, wet_upper, wet_lower = lax.psum(
        (source_upper, source_lower, target_upper, target_lower, wet_upper, wet_lower),
        ("lat", "lon"),
    )
    source = join_units(source_upper, source_lower)
    target = join_units(target_upper, target_lower)
    wet_area = join_units(wet_upper, wet_lower)
    correction = (source - target) / wet_area
    scaling = jnp.left_shift(jnp.ones_like(exponent), exponent).astype(jnp.float32)
    ocean_flux = (
        wet_cover * scaling[:, None, None] * (mapped / ocean_area + correction[:, None, None])
    )
    return (ocean_flux, source * scaling)


def solution(mesh):
    placed = (
        P(("member", "lat"), "lon", None, None),
        P(("member", "lat"), "lon", None),
        P(("member", "lat"), "lon", None),
        P(("member", "lat"), "lon", None),
        P(("member", "lat"), "lon"),
        P(("member", "lat"), "lon"),
        P(("member", "lat"), "lon"),
        P(),
    )
    return jax.shard_map(
        body,
        mesh=mesh,
        in_specs=placed,
        out_specs=(P(None, ("member", "lat"), "lon"), P("member")),
        check_vma=False,
    )
```

profile of v0, /device:TPU:0, one launch (start us, length us, event | category | flops | bytes accessed | tf_op | source)
XLA Modules:
  0.0 37.0 jit_solution(16438708426224895348)
XLA Ops:
  0.6 0.7 %fusion.29 = s32[16]{0:T(128)S(1)} fusion(s32[1,16]{1,0:T(1,128)} %param.12), kind=kLoop, calls=%fused_computation.62 | loop fusion | flops 240 | bytes 128 | tf_op jit(solution)/shard_map/eq | solution.py:38
  1.4 0.2 convert_reduce_fusion.2
  1.6 0.1 fusion
  1.7 0.7 %all_to_all.9 = f32[4,4,1]{1,0,2:T(4,128)} reshape(f32[16]{0:T(128)S(1)} %fusion) | data formatting | bytes 128 | tf_op jit(solution)/shard_map/all_to_all | solution.py:52
  2.4 6.3 %all-to-all-start = ((f32[4,4,1]{1,2,0:T(1,128)}), f32[4,4,1]{1,2,0:T(1,128)S(1)}, u32[]{:S(2)}, u32[]{:S(2)}) async-start(f32[4,4,1]{1,2,0:T(1,128)} %bitcast.6), calls=%async_computation | async-start | bytes 4096 | tf_op jit(solution)/shard_map/all_to_all | solution.py:52
  8.8 0.8 %multiply_bitcast_fusion.1 = f32[16,512]{1,0:T(8,128)S(1)} fusion(s32[1,16,512]{2,1,0:T(8,128)S(1)} %copy-done.3, f32[1,16,512]{2,1,0:T(8,128)} %param.11, f32[1,16,512]{2,1,0:T(8,128)} %param.9), kind=kLoop, calls=%fused_computation.14 | loop fusion | flops 24576 | bytes 131072 | tf_op jit(solution)/shard_map/mul | solution.py:31
  9.5 1.0 %multiply_bitcast_fusion = f32[16,8,512]{2,1,0:T(8,128)S(1)} fusion(f32[1,16,8,512]{3,2,1,0:T(8,128)} %param.8, f32[16,512]{1,0:T(8,128)S(1)} %multiply_bitcast_fusion.1), kind=kLoop, calls=%fused_computation.12 | loop fusion | flops 65536 | bytes 557056 | tf_op jit(solution)/shard_map/squeeze | solution.py:45
  10.6 0.4 %fusion.6 = f32[16,8,512]{2,0,1:T(8,128)S(1)} fusion(f32[16,8,512]{2,1,0:T(8,128)S(1)} %multiply_bitcast_fusion, s32[16]{0:T(128)S(1)} %fusion.21), kind=kOutput, calls=%fused_computation.8 | convolution fusion | flops 12583168 | bytes 524352 | tf_op jit(solution)/shard_map/qs,sfc->qfc/dot_general | solution.py:45
  11.0 0.2 copy-done.4
  11.2 0.1 copy-done.1
  11.3 0.6 %convert_reduce_fusion.1 = (s32[]{:T(128)}, f32[64,128]{1,0:T(8,128)S(1)}) fusion(f32[64,128]{1,0:T(8,128)S(1)} %copy-done.1, s32[64,128]{1,0:T(8,128)S(1)} %copy-done.2), kind=kLoop, calls=%fused_computation.13 | loop fusion | flops 40959 | bytes 98308 | tf_op jit(solution)/shard_map/reduce_sum | solution.py:11
  12.0 0.9 %copy.14 = f32[16,8,512]{2,1,0:T(8,128)} copy(f32[16,8,512]{2,0,1:T(8,128)S(1)} %fusion.6) | data formatting | bytes 524288 | tf_op jit(solution)/shard_map/qs,sfc->qfc/dot_general | solution.py:45
  12.8 1.4 %all-to-all-done = f32[4,4,1]{1,2,0:T(1,128)S(1)} async-done(((f32[4,4,1]{1,2,0:T(1,128)}), f32[4,4,1]{1,2,0:T(1,128)S(1)}, u32[]{:S(2)}, u32[]{:S(2)}) %all-to-all-start) | async-done | bytes 96 | tf_op jit(solution)/shard_map/all_to_all | solution.py:52
  14.2 3.9 %all-to-all-start.1 = ((f32[16,8,512]{2,1,0:T(8,128)}), f32[16,8,512]{2,1,0:T(8,128)S(1)}, u32[]{:S(2)}, u32[]{:S(2)}) async-start(f32[16,8,512]{2,1,0:T(8,128)} %copy.14), calls=%async_computation.1 | async-start | bytes 524288 | tf_op jit(solution)/shard_map/all_to_all | solution.py:51
  21.3 0.2 convert_reduce_fusion
  21.5 0.5 %broadcast.161 = f32[]{:T(128)} broadcast(f32[]{:T(128)} %constant.126), dimensions={} | broadcast | bytes 8 | tf_op jit(solution)/shard_map/all_to_all | solution.py:52
  22.0 0.7 %reduce.4 = f32[4,4]{1,0:T(4,128)S(1)} reduce(f32[4,4,1]{1,2,0:T(1,128)S(1)} %all-to-all-done, f32[]{:T(128)} %broadcast.161), dimensions={2}, to_apply=%all_to_all.10.reduce_sub_computation.3 | reduce | bytes 132 | tf_op jit(solution)/shard_map/all_to_all | solution.py:52
  22.8 3.6 %all-to-all-done.1 = f32[16,8,512]{2,1,0:T(8,128)S(1)} async-done(((f32[16,8,512]{2,1,0:T(8,128)}), f32[16,8,512]{2,1,0:T(8,128)S(1)}, u32[]{:S(2)}, u32[]{:S(2)}) %all-to-all-start.1) | async-done | bytes 262176 | tf_op jit(solution)/shard_map/all_to_all | solution.py:51
  26.4 0.4 %fusion.4 = f32[16,8,512]{2,0,1:T(8,128)S(1)} fusion(f32[16,8,512]{2,1,0:T(8,128)S(1)} %all-to-all-done.1, f32[16]{0:T(128)S(1)} %eq.52, f32[16]{0:T(128)S(1)} %iota_convert_fusion), kind=kOutput, calls=%fused_computation.6 | convolution fusion | flops 12583168 | bytes 524416 | tf_op jit(solution)/shard_map/nw,whl->nhl/dot_general | solution.py:57
  26.8 0.1 reshape.55
  26.9 0.3 fusion.3
  27.2 7.2 %all-reduce = (s32[8]{0:T(128)S(1)}, s32[8]{0:T(128)S(1)}, s32[]{:T(128)}, s32[]{:T(128)}, s32[8]{0:T(128)S(1)}, /*index=5*/s32[8]{0:T(128)S(1)}) all-reduce(s32[8]{0:T(128)S(1)} %get-tuple-element.10, s32[8]{0:T(128)S(1)} %get-tuple-element.11, s32[]{:T(128)S(6)} %select_n.37, ...), channel_id=1, replica_groups=mesh['member'=4,'lat'=2,'lon'=4] {'lat','lon'}, use_global_device_ids=true, to_apply=%region_6.7 | all-reduce | flops 34 | bytes 272 | tf_op jit(solution)/shard_map/psum | solution.py:67
  35.7 0.5 %fusion.28 = (f32[8]{0:T(128)}, f32[8]{0:T(128)S(1)}) fusion(s32[8]{0:T(128)S(1)} %copy-done.4, s32[8]{0:T(128)S(1)} %get-tuple-element.6, s32[8]{0:T(128)S(1)} %get-tuple-element.7, f32[]{:T(128)S(6)} %div.93, s32[8]{0:T(128)S(1)} %get-tuple-element.2, s32[8]{0:T(128)S(1)} %get-tuple-element.3), kind=kLoop, calls=%fused_computation.61 | loop fusion | flops 120 | bytes 228 | tf_op jit(solution)/shard_map/mul | solution.py:79
  36.2 0.8 %add_multiply_fusion = f32[8,64,128]{2,1,0:T(8,128)} fusion(f32[8,64,128]{2,1,0:T(8,128)S(1)} %bitcast.56, f32[8]{0:T(128)S(1)} %get-tuple-element.15, f32[64,128]{1,0:T(8,128)S(1)} %copy-done.1, f32[8]{0:T(128)S(1)} %shift-left_convert_fusion, f32[64,128]{1,0:T(8,128)S(1)} %get-tuple-element.13), kind=kLoop, calls=%fused_computation.10 | loop fusion | flops 262144 | bytes 589888 | tf_op jit(solution)/shard_map/mul | solution.py:77
  (17 shorter events, 0.2 us)
Async XLA Ops:
  0.6 0.7 %copy-start.5 = (s32[1,16]{1,0:T(1,128)S(1)}, s32[1,16]{1,0:T(1,128)}, u32[]{:S(2)}) copy-start(s32[1,16]{1,0:T(1,128)} %param.12) | copy-start | bytes 196
  0.6 8.1 %copy-start.3 = (s32[1,16,512]{2,1,0:T(8,128)S(1)}, s32[1,16,512]{2,1,0:T(8,128)}, u32[]{:S(2)}) copy-start(s32[1,16,512]{2,1,0:T(8,128)} %param.10) | copy-start | bytes 98308
  2.4 11.8 %all-to-all-start = ((f32[4,4,1]{1,2,0:T(1,128)}), f32[4,4,1]{1,2,0:T(1,128)S(1)}, u32[]{:S(2)}, u32[]{:S(2)}) async-start(f32[4,4,1]{1,2,0:T(1,128)} %bitcast.6), calls=%async_computation | async-start | bytes 4096 | tf_op jit(solution)/shard_map/all_to_all | solution.py:52
  10.5 0.7 %copy-start.4 = (s32[8]{0:T(128)S(1)}, s32[8]{0:T(128)}, u32[]{:S(2)}) copy-start(s32[8]{0:T(128)} %param.15) | copy-start | bytes 100
  10.5 0.8 %copy-start.1 = (f32[64,128]{1,0:T(8,128)S(1)}, f32[64,128]{1,0:T(8,128)}, u32[]{:S(2)}) copy-start(f32[64,128]{1,0:T(8,128)} %param.13) | copy-start | bytes 98308
  10.6 0.8 %copy-start.2 = (s32[64,128]{1,0:T(8,128)S(1)}, s32[64,128]{1,0:T(8,128)}, u32[]{:S(2)}) copy-start(s32[64,128]{1,0:T(8,128)} %param.14) | copy-start | bytes 98308
  12.8 8.5 %copy-start = (f32[1,16,8,512]{3,2,1,0:T(8,128)S(1)}, f32[1,16,8,512]{3,2,1,0:T(8,128)}, u32[]{:S(2)}) copy-start(f32[1,16,8,512]{3,2,1,0:T(8,128)} %param.8) | copy-start | bytes 786436
  14.2 12.2 %all-to-all-start.1 = ((f32[16,8,512]{2,1,0:T(8,128)}), f32[16,8,512]{2,1,0:T(8,128)S(1)}, u32[]{:S(2)}, u32[]{:S(2)}) async-start(f32[16,8,512]{2,1,0:T(8,128)} %copy.14), calls=%async_computation.1 | async-start | bytes 524288 | tf_op jit(solution)/shard_map/all_to_all | solution.py:51
where the time goes:
time: 37.6 us; the launch traced here: 37 us
  starting transfers between devices  10.2 us (27%)
  blocking collectives  7.23 us (19%)
  other arithmetic  5.81 us (15%)
  between operations  5.28 us (14%)
  waiting for transfers between devices  4.93 us (13%)
  local copies, waits for them, and re-layouts  2.61 us (7%)
  matrix products  0.94 us (2%)
    psum x1, blocking collectives, body(): lax.psum((source_upper, source_lower, target_upper, target_lower, wet_upp...  7.23 us
    all_to_all x1, starting transfers between devices, body(): lax.all_to_all(outgoing_rows, 'lon', split_axis=0, concat_axis=0, tiled=T...  6.35 us
    all_to_all x1, starting transfers between devices, body(): lax.all_to_all(outgoing, 'lon', split_axis=0, concat_axis=0, tiled=True)  3.88 us
    all_to_all x1, waiting for transfers between devices, body(): lax.all_to_all(outgoing, 'lon', split_axis=0, concat_axis=0, tiled=True)  3.58 us
    all_to_all x1, waiting for transfers between devices, body(): lax.all_to_all(outgoing_rows, 'lon', split_axis=0, concat_axis=0, tiled=T...  1.35 us
    all_to_all x2, local copies, waits for them, and re-layouts, body(): lax.all_to_all(outgoing_rows, 'lon', split_axis=0, concat_axis=0, tiled=T...  1.21 us
    reduce_sum x3, other arithmetic, local_units(): return jnp.sum((values * quantum).astype(jnp.int32), axis=axes)  1.1 us
    squeeze x1, other arithmetic, body(): carried[0]  0.98 us
  transfers between devices with their start and end apart: 2, of which 2 were waited for; matrix products, arithmetic and copies ran while one was open for 14% of the time, Pallas kernels for 0%

commit v1 on v0

v1 whole, which is shorter than its diff:
```python
import functools

import jax
import jax.numpy as jnp
from jax import lax
from jax.experimental import pallas as pl
from jax.experimental.pallas import tpu as pltpu
from jax.sharding import PartitionSpec as P

MESH = pl.DeviceIdType.MESH
quantum = 1024.0
limb_bits = 16
limb_base = 65536.0
lanes = 128


def carry(upper, lower):
    over = jnp.floor(lower * (1.0 / limb_base))
    return upper + over, lower - over * limb_base


def row_limbs(units):
    upper = jnp.sum((units >> limb_bits).astype(jnp.float32), axis=1, keepdims=True)
    lower = jnp.sum((units & 0xFFFF).astype(jnp.float32), axis=1, keepdims=True)
    return carry(upper, lower)


def join(upper, lower):
    return (upper * limb_base + lower) / quantum


def peer_order(count):
    return sorted(range(1, count), key=lambda d: (-min(d, count - d), -d))


def kernel(
    n_lat, n_lon, cap,
    flux_hbm, frac_hbm, mask_hbm, area_hbm, route_hbm, sea_hbm, wet_hbm, exp_hbm,
    out_ref, total_ref,
    flux, frac, mask, area, sea, wet, wetf, inverse, outgoing, received, routes, exps, sums,
    in_sem, route_send, route_recv, bulk_send, bulk_recv, sum_send, sum_recv,
):
    blocks, fields, cells = flux.shape
    rows, width = sea.shape
    band = cells // width
    bits = blocks.bit_length()
    digit = (1 << bits) - 1
    full = cap * n_lon == blocks
    group = n_lat * n_lon
    my_lat = lax.axis_index("lat")
    me = lax.axis_index("lon")

    def peer(offset):
        return {
            "lat": lax.rem(my_lat + offset // n_lon, n_lat),
            "lon": lax.rem(me + offset % n_lon, n_lon),
        }

    loads = [
        pltpu.make_async_copy(src, dst, in_sem.at[i])
        for i, (src, dst) in enumerate((
            (route_hbm, routes.at[pl.ds(0, 1)]), (area_hbm, area), (frac_hbm, frac),
            (mask_hbm, mask), (flux_hbm, flux), (sea_hbm, sea), (wet_hbm, wet), (exp_hbm, exps),
        ))
    ]
    for load in loads:
        load.start()

    barrier = pltpu.get_barrier_semaphore()
    for offset in range(1, group):
        pl.semaphore_signal(barrier, inc=1, device_id=peer(offset), device_id_type=MESH)

    loads[0].wait()

    def digits_of(slot, low, value):
        packed = jnp.int32(0)
        for s in range(blocks):
            r = routes[slot, s]
            hit = (r >= low) & (r < low + blocks)
            packed = jnp.where(hit, (packed << bits) + (value(s, r - low) + 1), packed)
        return [(packed >> (bits * (cap - 1 - c))) & digit for c in range(cap)]

    chosen = {}
    order = peer_order(n_lon) + [0]
    for d in order:
        low = lax.rem(me + d, n_lon) * blocks
        chosen[d] = [jnp.maximum(v - 1, 0) for v in digits_of(0, low, lambda s, row: s)]

    for load in loads[1:5]:
        load.wait()
    pl.semaphore_wait(barrier, group - 1)

    route_copies = {}
    for d in order[:-1]:
        route_copies[d] = pltpu.make_async_remote_copy(
            src_ref=route_hbm, dst_ref=routes.at[pl.ds(d, 1)],
            send_sem=route_send.at[d - 1], recv_sem=route_recv.at[d - 1],
            device_id=peer(d), device_id_type=MESH,
        )
        route_copies[d].start()

    bulk = {}
    for d in order:
        for c in range(cap):
            s = chosen[d][c]
            here = pl.ds(s, 1)
            amount = area[here, :] * frac[here, :] * mask[here, :].astype(jnp.float32)
            block = flux[s] * amount
            if d:
                outgoing[(d - 1) * cap + c] = block
            else:
                received[c] = block
        if d:
            bulk[d] = pltpu.make_async_remote_copy(
                src_ref=outgoing.at[pl.ds((d - 1) * cap, cap)],
                dst_ref=received.at[pl.ds(d * cap, cap)],
                send_sem=bulk_send.at[d - 1], recv_sem=bulk_recv.at[d - 1],
                device_id=peer(d), device_id_type=MESH,
            )
            bulk[d].start()

    source_units = jnp.zeros((fields, width), jnp.int32)
    for s in range(blocks):
        here = pl.ds(s, 1)
        amount = area[here, :] * frac[here, :] * mask[here, :].astype(jnp.float32)
        units = (flux[s] * amount * quantum).astype(jnp.int32)
        for r in range(band):
            source_units += units[:, r * width : (r + 1) * width]

    for load in loads[5:]:
        load.wait()
    wetf[...] = wet[...].astype(jnp.float32)
    inverse[...] = wetf[...] / sea[...]
    area_units = jnp.zeros((8, width), jnp.int32)
    for i in range(rows // 8):
        part = pl.ds(i * 8, 8)
        area_units += (sea[part, :] * wetf[part, :] * quantum).astype(jnp.int32)

    sub = lax.broadcasted_iota(jnp.int32, (8, lanes), 0)
    lane = lax.broadcasted_iota(jnp.int32, (8, lanes), 1)

    def placed(values, first):
        return sum(
            jnp.where(lane == sub + (first + i) * 8, v, 0.0) for i, v in enumerate(values)
        )

    early = placed(row_limbs(source_units) + row_limbs(area_units), 0)
    power = jnp.zeros((8, lanes), jnp.int32)
    power_row = jnp.zeros((1, lanes), jnp.int32)
    for f in range(fields):
        power = jnp.where(sub == f, exps[f], power)
        power_row = jnp.where(lane[:1] == f, exps[f], power_row)
    scaling = jnp.left_shift(jnp.ones_like(power), power).astype(jnp.float32)
    scaling_row = jnp.left_shift(jnp.ones_like(power_row), power_row).astype(jnp.float32)

    low = me * blocks
    slot_of = [jnp.int32(0)] * blocks
    target_units = jnp.zeros((fields, width), jnp.int32)
    for d in [0] + order[:-1]:
        if d:
            route_copies[d].wait_recv()
        digits = digits_of(d, low, lambda s, row: row)
        for c in range(cap):
            for n in range(blocks):
                slot_of[n] = jnp.where(digits[c] == n + 1, d * cap + c, slot_of[n])
        if d:
            bulk[d].wait_recv()
        for c in range(cap):
            row = jnp.maximum(digits[c] - 1, 0)
            for r in range(band):
                cover = wetf[pl.ds(row * band + r, 1), :]
                value = received[d * cap + c, :, r * width : (r + 1) * width]
                units = (cover * value * quantum).astype(jnp.int32)
                if not full:
                    units = units * jnp.minimum(digits[c], 1)
                target_units += units

    mine = jnp.sum(early + placed(row_limbs(target_units), 4), axis=0, keepdims=True)
    sums[pl.ds(0, 1), :] = mine
    sum_copies = []
    for offset in range(1, group):
        copy = pltpu.make_async_remote_copy(
            src_ref=sums.at[pl.ds(0, 1)], dst_ref=sums.at[pl.ds(offset, 1)],
            send_sem=sum_send.at[offset - 1], recv_sem=sum_recv.at[offset - 1],
            device_id=peer(offset), device_id_type=MESH,
        )
        copy.start()
        sum_copies.append(copy)
    for copy in sum_copies:
        copy.wait_recv()

    whole = jnp.sum(sums[...], axis=0, keepdims=True)

    def taken(i):
        return jnp.sum(jnp.where(lane == sub + i * 8, whole, 0.0), axis=1, keepdims=True)

    source = join(taken(0), taken(1))
    wet_upper, wet_lower = carry(taken(2), taken(3))
    wet_area = join(
        jnp.sum(wet_upper, axis=0, keepdims=True), jnp.sum(wet_lower, axis=0, keepdims=True)
    )
    target = join(taken(4), taken(5))
    offset_value = scaling * ((source - target) / wet_area)

    for n in range(blocks):
        slot = slot_of[n]
        for r in range(band):
            line = n * band + r
            value = received[slot, :, r * width : (r + 1) * width]
            result = scaling * (value * inverse[line : line + 1, :])
            result = result + offset_value * wetf[line : line + 1, :]
            out_ref[pl.ds(line, fields, stride=rows), :] = result

    aligned = pltpu.roll(whole, lanes - 8, 1)
    total_ref[...] = join(whole, aligned) * scaling_row

    for copy in sum_copies:
        copy.wait_send()
    for d in order[:-1]:
        route_copies[d].wait_send()
        bulk[d].wait_send()


def solution(mesh):
    n_lat, n_lon = mesh.shape["lat"], mesh.shape["lon"]

    def body(ice_flux, ice_frac, ice_mask, ice_area, route, ocean_area, ocean_wet, exponent):
        blocks, fields, cells = ice_flux.shape[1:]
        rows, width = ocean_area.shape
        cap = max(2, blocks // n_lon)
        group = n_lat * n_lon
        anywhere = pl.BlockSpec(memory_space=pl.ANY)
        vmem = pl.BlockSpec(memory_space=pltpu.VMEM)
        dma = pltpu.SemaphoreType.DMA
        flux_out, total = pl.pallas_call(
            functools.partial(kernel, n_lat, n_lon, cap),
            out_shape=(
                jax.ShapeDtypeStruct((fields * rows, width), jnp.float32),
                jax.ShapeDtypeStruct((1, lanes), jnp.float32),
            ),
            in_specs=[anywhere] * 8,
            out_specs=(vmem, vmem),
            scratch_shapes=[
                pltpu.VMEM((blocks, fields, cells), jnp.float32),
                pltpu.VMEM((blocks, cells), jnp.float32),
                pltpu.VMEM((blocks, cells), jnp.int32),
                pltpu.VMEM((blocks, cells), jnp.float32),
                pltpu.VMEM((rows, width), jnp.float32),
                pltpu.VMEM((rows, width), jnp.int32),
                pltpu.VMEM((rows, width), jnp.float32),
                pltpu.VMEM((rows, width), jnp.float32),
                pltpu.VMEM(((n_lon - 1) * cap, fields, cells), jnp.float32),
                pltpu.VMEM((n_lon * cap, fields, cells), jnp.float32),
                pltpu.SMEM((n_lon, blocks), jnp.int32),
                pltpu.SMEM((fields,), jnp.int32),
                pltpu.VMEM((group, lanes), jnp.float32),
                dma((8,)),
                dma((n_lon - 1,)), dma((n_lon - 1,)),
                dma((n_lon - 1,)), dma((n_lon - 1,)),
                dma((group - 1,)), dma((group - 1,)),
            ],
            compiler_params=pltpu.CompilerParams(collective_id=0, has_side_effects=True),
        )(
            ice_flux[0], ice_frac[0], ice_mask[0], ice_area[0],
            route, ocean_area, ocean_wet, exponent,
        )
        return flux_out.reshape(fields, rows, width), total[0, :fields]

    placed = (
        P(("member", "lat"), "lon", None, None),
        P(("member", "lat"), "lon", None),
        P(("member", "lat"), "lon", None),
        P(("member", "lat"), "lon", None),
        P(("member", "lat"), "lon"),
        P(("member", "lat"), "lon"),
        P(("member", "lat"), "lon"),
        P(),
    )
    return jax.shard_map(
        body,
        mesh=mesh,
        in_specs=placed,
        out_specs=(P(None, ("member", "lat"), "lon"), P("member")),
        check_vma=False,
    )
```

time: 37.6 us -> 20.8 us (0.55); the launches traced: 37 us -> 20.6 us
  Pallas kernels: 0 us -> 17.3 us
  starting transfers between devices: 10.2 us -> 0 us
  blocking collectives: 7.23 us -> 0 us
  other arithmetic: 5.81 us -> 0 us
  waiting for transfers between devices: 4.93 us -> 0 us
  between operations: 5.28 us -> 0.65 us
  matrix products: 0.94 us -> 0 us
    pallas_call x0 -> x1, Pallas kernels: none -> 17.3 us  [body(): pl.pallas_call(functools.partial(kernel, n_lat, n_lon, cap), out_shape=(j...]
    all_to_all x2 -> x0, starting transfers between devices: 10.2 us -> none  [the longest x1 6.35 us: body(): lax.all_to_all(outgoing_rows, 'lon', split_axis=0, concat_axis=0, tiled=T...]
    psum x1 -> x0, blocking collectives: 7.23 us -> none  [body(): lax.psum((source_upper, source_lower, target_upper, target_lower, wet_upp...]
    all_to_all x2 -> x0, waiting for transfers between devices: 4.93 us -> none  [the longest x1 3.58 us: body(): lax.all_to_all(outgoing, 'lon', split_axis=0, concat_axis=0, tiled=True)]
    mul x3 -> x0, other arithmetic: 2.1 us -> none  [the longest x1 0.8 us: body(): wet_cover * scaling[:, None, None]]
    unnamed x12 -> x3, local copies, waits for them, and re-layouts: 0.36 us -> 2.24 us
    reduce_sum x4 -> x0, other arithmetic: 1.28 us -> none  [the longest x3 1.1 us: local_units(): return jnp.sum((values * quantum).astype(jnp.int32), axis=axes)]
    all_to_all x2 -> x0, local copies, waits for them, and re-layouts: 1.21 us -> none  [body(): lax.all_to_all(outgoing_rows, 'lon', split_axis=0, concat_axis=0, tiled=T...]
  transfers between devices with their start and end apart: 2 -> 0, of which waited for: 2 -> 0; matrix products, arithmetic and copies ran while one was open for 14% -> 0% of each run, Pallas kernels for 0% -> 0%
where the time goes in v1:
time: 20.8 us; the launch traced here: 20.6 us
  Pallas kernels  17.3 us (83%)
  local copies, waits for them, and re-layouts  2.75 us (13%)
  between operations  0.65 us (3%)
    pallas_call x1, Pallas kernels, body(): pl.pallas_call(functools.partial(kernel, n_lat, n_lon, cap), out_shape=(j...  17.3 us
    unnamed x3, local copies, waits for them, and re-layouts  2.24 us
    squeeze x1, local copies, waits for them, and re-layouts, body(): return (flux_out.reshape(fields, rows, width), total[0, :fields])  0.51 us

profile of v1, /device:TPU:0, one launch (start us, length us, event | category | flops | bytes accessed | tf_op | source)
XLA Modules:
  0.0 20.6 jit_solution(9397114570270039487)
XLA Ops:
  0.6 17.3 %shard_map.95 = (f32[512,128]{1,0:T(8,128)}, f32[1,128]{1,0:T(1,128)}) custom-call(f32[16,8,512]{2,1,0:T(8,128)} %bitcast.8, f32[16,512]{1,0:T(8,128)} %bitcast.9, s32[16,512]{1,0:T(8,128)} %bitcast.10, f32[16,512]{1,0:T(8,128)} %bitcast.11, s32[1,16]{1,0:T(1,128)} %route_hbm.1, f32[64,128]{1,0:T(8,128)} %sea_hbm.1, s32[64,128]{1,0:T(8,128)} %wet_hbm.1, ...), custom_call_target="tpu_custom_call" | custom-call | tf_op jit(solution)/shard_map/pallas_call | solution.py:235
  17.9 0.0 copy-start
  17.9 0.6 %copy-done = f32[1,128]{1,0:T(1,128)S(1)} copy-done((f32[1,128]{1,0:T(1,128)S(1)}, f32[1,128]{1,0:T(1,128)}, u32[]{:S(2)}) %copy-start) | copy-done | bytes 536
  18.5 0.5 %slice_bitcast_fusion = f32[8]{0:T(128)} fusion(f32[1,128]{1,0:T(1,128)S(1)} %copy-done), kind=kLoop, calls=%fused_computation | loop fusion | bytes 64 | tf_op jit(solution)/shard_map/squeeze | solution.py:267
  19.0 1.7 %copy.11 = f32[8,64,128]{2,1,0:T(8,128)} copy(f32[8,64,128]{2,1,0:T(8,128)} %bitcast.7) | data formatting | bytes 524288
Async XLA Ops:
  17.9 0.6 %copy-start = (f32[1,128]{1,0:T(1,128)S(1)}, f32[1,128]{1,0:T(1,128)}, u32[]{:S(2)}) copy-start(f32[1,128]{1,0:T(1,128)} %get-tuple-element.5) | copy-start | bytes 1540

commit v2 on v1

--- a/solution.py
+++ b/solution.py
@@ -29,15 +29,19 @@
     return (upper * limb_base + lower) / quantum
 
 
-def peer_order(count):
-    return sorted(range(1, count), key=lambda d: (-min(d, count - d), -d))
+def send_steps(count):
+    table = []
+    for me in range(count):
+        near = sorted((p for p in range(count) if p != me), key=lambda p: (abs(p - me), p))
+        table.append(near[-1:] + near[:-1])
+    return [[row[step] for row in table] for step in range(count - 1)]
 
 
 def kernel(
     n_lat, n_lon, cap,
     flux_hbm, frac_hbm, mask_hbm, area_hbm, route_hbm, sea_hbm, wet_hbm, exp_hbm,
-    out_ref, total_ref,
-    flux, frac, mask, area, sea, wet, wetf, inverse, outgoing, received, routes, exps, sums,
+    ordered, wetf, coefs, total_ref,
+    flux, frac, mask, area, sea, wet, inverse, outgoing, received, routes, exps, sums,
     in_sem, route_send, route_recv, bulk_send, bulk_recv, sum_send, sum_recv,
 ):
     blocks, fields, cells = flux.shape
@@ -80,44 +84,67 @@
             packed = jnp.where(hit, (packed << bits) + (value(s, r - low) + 1), packed)
         return [(packed >> (bits * (cap - 1 - c))) & digit for c in range(cap)]
 
-    chosen = {}
-    order = peer_order(n_lon) + [0]
-    for d in order:
-        low = lax.rem(me + d, n_lon) * blocks
-        chosen[d] = [jnp.maximum(v - 1, 0) for v in digits_of(0, low, lambda s, row: s)]
-
+    pl.semaphore_wait(barrier, group - 1)
+
+    if n_lon ** n_lon < 2 ** 31:
+        place = 1
+        for i in range(n_lon - 1):
+            place = place * (1 + (n_lon - 1) * ((me + n_lon - 1 - i) // n_lon))
+        steps = [
+            sum(t * n_lon ** i for i, t in enumerate(row)) // place % n_lon
+            for row in send_steps(n_lon)
+        ]
+    else:
+        steps = [lax.rem(me + d, n_lon) for d in range(1, n_lon)]
+    away = [lax.rem(target - me + n_lon, n_lon) for target in steps]
+
+    def lon_copy(src, dst, send, recv, d, target):
+        return pltpu.make_async_remote_copy(
+            src_ref=src, dst_ref=dst, send_sem=send.at[d - 1], recv_sem=recv.at[d - 1],
+            device_id={"lat": my_lat, "lon": target}, device_id_type=MESH,
+        )
+
+    route_copies = [
+        lon_copy(routes.at[pl.ds(0, 1)], routes.at[pl.ds(d, 1)], route_send, route_recv, d, t)
+        for d, t in zip(away, steps)
+    ]
+    for copy in route_copies:
+        copy.start()
+
+    chosen = [
+        [jnp.maximum(v - 1, 0) for v in digits_of(0, target * blocks, lambda s, row: s)]
+        for target in steps + [me]
+    ]
     for load in loads[1:5]:
         load.wait()
-    pl.semaphore_wait(barrier, group - 1)
-
-    route_copies = {}
-    for d in order[:-1]:
-        route_copies[d] = pltpu.make_async_remote_copy(
-            src_ref=route_hbm, dst_ref=routes.at[pl.ds(d, 1)],
-            send_sem=route_send.at[d - 1], recv_sem=route_recv.at[d - 1],
-            device_id=peer(d), device_id_type=MESH,
-        )
-        route_copies[d].start()
-
-    bulk = {}
-    for d in order:
-        for c in range(cap):
-            s = chosen[d][c]
+
+    bulk = []
+    for step, picks in enumerate(chosen):
+        last = step == n_lon - 1
+        for c, s in enumerate(picks):
             here = pl.ds(s, 1)
             amount = area[here, :] * frac[here, :] * mask[here, :].astype(jnp.float32)
             block = flux[s] * amount
-            if d:
-                outgoing[(d - 1) * cap + c] = block
+            if last:
+                received[c] = block
             else:
-                received[c] = block
-        if d:
-            bulk[d] = pltpu.make_async_remote_copy(
-                src_ref=outgoing.at[pl.ds((d - 1) * cap, cap)],
-                dst_ref=received.at[pl.ds(d * cap, cap)],
-                send_sem=bulk_send.at[d - 1], recv_sem=bulk_recv.at[d - 1],
-                device_id=peer(d), device_id_type=MESH,
-            )
-            bulk[d].start()
+                outgoing[step * cap + c] = block
+        if not last:
+            d = away[step]
+            bulk.append(lon_copy(
+                outgoing.at[pl.ds(step * cap, cap)], received.at[pl.ds(d * cap, cap)],
+                bulk_send, bulk_recv, d, steps[step],
+            ))
+            bulk[-1].start()
+
+    def arrival(d):
+        here = received.at[pl.ds(d * cap, cap)]
+        line = routes.at[pl.ds(d, 1)]
+        source = lax.rem(me - d + n_lon, n_lon)
+        return (
+            lon_copy(line, line, route_send, route_recv, d, source),
+            lon_copy(here, here, bulk_send, bulk_recv, d, source),
+        )
 
     source_units = jnp.zeros((fields, width), jnp.int32)
     for s in range(blocks):
@@ -156,15 +183,17 @@
     low = me * blocks
     slot_of = [jnp.int32(0)] * blocks
     target_units = jnp.zeros((fields, width), jnp.int32)
-    for d in [0] + order[:-1]:
+    near_first = sorted(range(n_lon), key=lambda d: min(d, n_lon - d))
+    for d in near_first:
         if d:
-            route_copies[d].wait_recv()
+            route_arrival, bulk_arrival = arrival(d)
+            route_arrival.wait_recv()
         digits = digits_of(d, low, lambda s, row: row)
         for c in range(cap):
             for n in range(blocks):
                 slot_of[n] = jnp.where(digits[c] == n + 1, d * cap + c, slot_of[n])
         if d:
-            bulk[d].wait_recv()
+            bulk_arrival.wait_recv()
         for c in range(cap):
             row = jnp.maximum(digits[c] - 1, 0)
             for r in range(band):
@@ -186,6 +215,13 @@
         )
         copy.start()
         sum_copies.append(copy)
+    for n in range(blocks):
+        slot = slot_of[n]
+        for r in range(band):
+            line = n * band + r
+            value = received[slot, :, r * width : (r + 1) * width]
+            ordered[pl.ds(line, fields, stride=rows), :] = value * inverse[line : line + 1, :]
+
     for copy in sum_copies:
         copy.wait_recv()
 
@@ -200,25 +236,28 @@
         jnp.sum(wet_upper, axis=0, keepdims=True), jnp.sum(wet_lower, axis=0, keepdims=True)
     )
     target = join(taken(4), taken(5))
-    offset_value = scaling * ((source - target) / wet_area)
-
-    for n in range(blocks):
-        slot = slot_of[n]
-        for r in range(band):
-            line = n * band + r
-            value = received[slot, :, r * width : (r + 1) * width]
-            result = scaling * (value * inverse[line : line + 1, :])
-            result = result + offset_value * wetf[line : line + 1, :]
-            out_ref[pl.ds(line, fields, stride=rows), :] = result
+    coefs[0] = scaling
+    coefs[1] = scaling * ((source - target) / wet_area)
 
     aligned = pltpu.roll(whole, lanes - 8, 1)
     total_ref[...] = join(whole, aligned) * scaling_row
 
-    for copy in sum_copies:
+    for copy in sum_copies + route_copies + bulk:
         copy.wait_send()
-    for d in order[:-1]:
-        route_copies[d].wait_send()
-        bulk[d].wait_send()
+
+
+def finish(ordered, wetf, coefs, total_row, out_hbm, total_ref, out, sems):
+    fields = total_ref.shape[0]
+    rows = wetf.shape[0]
+    copies = []
+    for f in range(fields):
+        here = pl.ds(f * rows, rows)
+        out[here, :] = ordered[here, :] * coefs[0, f : f + 1, :] + wetf[...] * coefs[1, f : f + 1, :]
+        copies.append(pltpu.make_async_copy(out.at[here], out_hbm.at[here], sems.at[f]))
+        copies[-1].start()
+    total_ref[...] = total_row[0, :fields]
+    for copy in copies:
+        copy.wait()
 
 
 def solution(mesh):
@@ -232,14 +271,16 @@
         anywhere = pl.BlockSpec(memory_space=pl.ANY)
         vmem = pl.BlockSpec(memory_space=pltpu.VMEM)
         dma = pltpu.SemaphoreType.DMA
-        flux_out, total = pl.pallas_call(
+        near = pl.pallas_call(
             functools.partial(kernel, n_lat, n_lon, cap),
             out_shape=(
-                jax.ShapeDtypeStruct((fields * rows, width), jnp.float32),
-                jax.ShapeDtypeStruct((1, lanes), jnp.float32),
+                pltpu.VMEM((fields * rows, width), jnp.float32),
+                pltpu.VMEM((rows, width), jnp.float32),
+                pltpu.VMEM((2, fields, lanes), jnp.float32),
+                pltpu.VMEM((1, lanes), jnp.float32),
             ),
             in_specs=[anywhere] * 8,
-            out_specs=(vmem, vmem),
+            out_specs=(vmem,) * 4,
             scratch_shapes=[
                 pltpu.VMEM((blocks, fields, cells), jnp.float32),
                 pltpu.VMEM((blocks, cells), jnp.float32),
@@ -247,7 +288,6 @@
                 pltpu.VMEM((blocks, cells), jnp.float32),
                 pltpu.VMEM((rows, width), jnp.float32),
                 pltpu.VMEM((rows, width), jnp.int32),
-                pltpu.VMEM((rows, width), jnp.float32),
                 pltpu.VMEM((rows, width), jnp.float32),
                 pltpu.VMEM(((n_lon - 1) * cap, fields, cells), jnp.float32),
                 pltpu.VMEM((n_lon * cap, fields, cells), jnp.float32),
@@ -264,7 +304,17 @@
             ice_flux[0], ice_frac[0], ice_mask[0], ice_area[0],
             route, ocean_area, ocean_wet, exponent,
         )
-        return flux_out.reshape(fields, rows, width), total[0, :fields]
+        flux_out, total = pl.pallas_call(
+            finish,
+            out_shape=(
+                jax.ShapeDtypeStruct((fields * rows, width), jnp.float32),
+                jax.ShapeDtypeStruct((fields,), jnp.float32),
+            ),
+            in_specs=[vmem] * 4,
+            out_specs=(anywhere, vmem),
+            scratch_shapes=[pltpu.VMEM((fields * rows, width), jnp.float32), dma((fields,))],
+        )(*(pltpu.with_memory_space_constraint(x, pltpu.VMEM) for x in near))
+        return flux_out.reshape(fields, rows, width), total
 
     placed = (
         P(("member", "lat"), "lon", None, None),

time: 20.8 us -> 18.3 us (0.88)
  local copies, waits for them, and re-layouts: 2.75 us -> 0 us
    unnamed x3 -> x0, local copies, waits for them, and re-layouts: 2.24 us -> none
    squeeze x1 -> x0, local copies, waits for them, and re-layouts: 0.51 us -> none  [body(): return (flux_out.reshape(fields, rows, width), total[0, :fields])]
    pallas_call x1 -> x2, Pallas kernels: 17.3 us -> 17.5 us  [the longest x1 16.2 us: body(): pl.pallas_call(functools.partial(kernel, n_lat, n_lon, cap), out_shape=(p...]
where the time goes in v2:
time: 18.3 us; the launch traced here: 18.1 us
  Pallas kernels  17.5 us (96%)
  between operations  0.64 us (3%)
    pallas_call x1, Pallas kernels, body(): pl.pallas_call(functools.partial(kernel, n_lat, n_lon, cap), out_shape=(p...  16.2 us
    pallas_call x1, Pallas kernels, body(): pl.pallas_call(finish, out_shape=(jax.ShapeDtypeStruct((fields * rows, wi...  1.28 us

profile of v2, /device:TPU:0, one launch (start us, length us, event | category | flops | bytes accessed | tf_op | source)
XLA Modules:
  0.0 18.1 jit_solution(3545388544071018835)
XLA Ops:
  0.6 16.2 %shard_map.95 = (f32[512,128]{1,0:T(8,128)S(1)}, f32[64,128]{1,0:T(8,128)S(1)}, f32[2,8,128]{2,1,0:T(8,128)S(1)}, f32[1,128]{1,0:T(1,128)S(1)}) custom-call(f32[16,8,512]{2,1,0:T(8,128)} %bitcast.5, f32[16,512]{1,0:T(8,128)} %bitcast.6, s32[16,512]{1,0:T(8,128)} %bitcast.7, f32[16,512]{1,0:T(8,128)} %bitcast.8, s32[1,16]{1,0:T(1,128)} %route_hbm.1, ...), custom_call_target="tpu_custom_call" | custom-call | tf_op jit(solution)/shard_map/pallas_call | solution.py:274
  16.8 1.3 %shard_map.96 = (f32[512,128]{1,0:T(8,128)}, f32[8]{0:T(128)}) custom-call(f32[512,128]{1,0:T(8,128)S(1)} %get-tuple-element.8.ordered, f32[64,128]{1,0:T(8,128)S(1)} %get-tuple-element.9.wetf, f32[2,8,128]{2,1,0:T(8,128)S(1)} %get-tuple-element.10.coefs, f32[1,128]{1,0:T(1,128)S(1)} %get-tuple-element.11.total_row), custom_call_target="tpu_custom_call" | custom-call | tf_op jit(solution)/shard_map/pallas_call | solution.py:307

commit v3 on v2

--- a/solution.py
+++ b/solution.py
@@ -29,20 +29,34 @@
     return (upper * limb_base + lower) / quantum
 
 
-def send_steps(count):
-    table = []
+def plan(count):
+    middle = (count - 1) / 2
+    sends = []
     for me in range(count):
-        near = sorted((p for p in range(count) if p != me), key=lambda p: (abs(p - me), p))
-        table.append(near[-1:] + near[:-1])
-    return [[row[step] for row in table] for step in range(count - 1)]
+        near = sorted(
+            (p for p in range(count) if p != me),
+            key=lambda p: (abs(p - me), -((p - me) * (middle - me) > 0)),
+        )
+        sends.append(near[-1:] + near[:-1])
+    late = [row[-1] for row in sends]
+    if count ** count >= 2 ** 31 or sorted(late) != list(range(count)):
+        return None
+    sources = []
+    for me in range(count):
+        last = late.index(me)
+        early = sorted(
+            (p for p in range(count) if p not in (me, last)), key=lambda p: abs(p - me)
+        )
+        sources.append(early + [last])
+    return sends, sources
 
 
 def kernel(
     n_lat, n_lon, cap,
     flux_hbm, frac_hbm, mask_hbm, area_hbm, route_hbm, sea_hbm, wet_hbm, exp_hbm,
     ordered, wetf, coefs, total_ref,
-    flux, frac, mask, area, sea, wet, inverse, outgoing, received, routes, exps, sums,
-    in_sem, route_send, route_recv, bulk_send, bulk_recv, sum_send, sum_recv,
+    flux, frac, mask, area, sea, wet, inverse, outgoing, received, routes, exps, sums, cover_out, cover_in,
+    in_sem, route_send, route_recv, bulk_send, bulk_recv, sum_send, sum_recv, cover_sem,
 ):
     blocks, fields, cells = flux.shape
     rows, width = sea.shape
@@ -84,67 +98,84 @@
             packed = jnp.where(hit, (packed << bits) + (value(s, r - low) + 1), packed)
         return [(packed >> (bits * (cap - 1 - c))) & digit for c in range(cap)]
 
-    pl.semaphore_wait(barrier, group - 1)
-
-    if n_lon ** n_lon < 2 ** 31:
+    planned = plan(n_lon)
+    if planned:
         place = 1
         for i in range(n_lon - 1):
             place = place * (1 + (n_lon - 1) * ((me + n_lon - 1 - i) // n_lon))
-        steps = [
-            sum(t * n_lon ** i for i, t in enumerate(row)) // place % n_lon
-            for row in send_steps(n_lon)
-        ]
+        steps, sources = (
+            [
+                sum(row[step] * n_lon ** i for i, row in enumerate(table)) // place % n_lon
+                for step in range(n_lon - 1)
+            ]
+            for table in planned
+        )
     else:
         steps = [lax.rem(me + d, n_lon) for d in range(1, n_lon)]
+        sources = [lax.rem(me + n_lon - d, n_lon) for d in range(1, n_lon)]
     away = [lax.rem(target - me + n_lon, n_lon) for target in steps]
-
-    def lon_copy(src, dst, send, recv, d, target):
+    behind = [lax.rem(me - source + n_lon, n_lon) for source in sources]
+
+    def lon_copy(src, dst, send, recv, target):
         return pltpu.make_async_remote_copy(
-            src_ref=src, dst_ref=dst, send_sem=send.at[d - 1], recv_sem=recv.at[d - 1],
+            src_ref=src, dst_ref=dst, send_sem=send, recv_sem=recv,
             device_id={"lat": my_lat, "lon": target}, device_id_type=MESH,
         )
 
-    route_copies = [
-        lon_copy(routes.at[pl.ds(0, 1)], routes.at[pl.ds(d, 1)], route_send, route_recv, d, t)
-        for d, t in zip(away, steps)
-    ]
-    for copy in route_copies:
-        copy.start()
-
-    chosen = [
-        [jnp.maximum(v - 1, 0) for v in digits_of(0, target * blocks, lambda s, row: s)]
-        for target in steps + [me]
-    ]
+    def route_copy(d, src, target):
+        return lon_copy(
+            routes.at[pl.ds(src, 1)], routes.at[pl.ds(d, 1)],
+            route_send.at[d - 1], route_recv.at[d - 1], target,
+        )
+
+    def bulk_copy(d, src, first, target):
+        return lon_copy(
+            src.at[pl.ds(first, cap)], received.at[pl.ds(d * cap, cap)],
+            bulk_send.at[d - 1], bulk_recv.at[d - 1], target,
+        )
+
+    def fill(target, dst, first):
+        picks = digits_of(0, target * blocks, lambda s, row: s)
+        for c, pick in enumerate(picks):
+            s = jnp.maximum(pick - 1, 0)
+            here = pl.ds(s, 1)
+            amount = area[here, :] * frac[here, :] * mask[here, :].astype(jnp.float32)
+            dst[first + c] = flux[s] * amount
+
     for load in loads[1:5]:
         load.wait()
-
-    bulk = []
-    for step, picks in enumerate(chosen):
-        last = step == n_lon - 1
-        for c, s in enumerate(picks):
-            here = pl.ds(s, 1)
-            amount = area[here, :] * frac[here, :] * mask[here, :].astype(jnp.float32)
-            block = flux[s] * amount
-            if last:
-                received[c] = block
-            else:
-                outgoing[step * cap + c] = block
-        if not last:
-            d = away[step]
-            bulk.append(lon_copy(
-                outgoing.at[pl.ds(step * cap, cap)], received.at[pl.ds(d * cap, cap)],
-                bulk_send, bulk_recv, d, steps[step],
-            ))
-            bulk[-1].start()
-
-    def arrival(d):
-        here = received.at[pl.ds(d * cap, cap)]
-        line = routes.at[pl.ds(d, 1)]
-        source = lax.rem(me - d + n_lon, n_lon)
-        return (
-            lon_copy(line, line, route_send, route_recv, d, source),
-            lon_copy(here, here, bulk_send, bulk_recv, d, source),
-        )
+    for step, target in enumerate(steps):
+        fill(target, outgoing, step * cap)
+
+    pl.semaphore_wait(barrier, group - 1)
+    route_copies = [route_copy(d, 0, target) for d, target in zip(away, steps)]
+    bulk = [
+        bulk_copy(d, outgoing, step * cap, target)
+        for step, (d, target) in enumerate(zip(away, steps))
+    ]
+    for copy in route_copies + bulk[:1]:
+        copy.start()
+    fill(me, received, 0)
+
+    for load in loads[5:]:
+        load.wait()
+    wetf[...] = wet[...].astype(jnp.float32)
+
+    low = me * blocks
+    last_source, last_behind = sources[-1], behind[-1]
+    route_copy(last_behind, last_behind, last_source).wait_recv()
+    last_digits = digits_of(last_behind, low, lambda s, row: row)
+    for c, pick in enumerate(last_digits):
+        row = jnp.maximum(pick - 1, 0)
+        for r in range(band):
+            cover = wetf[pl.ds(row * band + r, 1), :]
+            if not full:
+                cover = cover * jnp.minimum(pick, 1).astype(jnp.float32)
+            cover_out[pl.ds(c * band + r, 1), :] = cover
+    cover_copy = lon_copy(cover_out, cover_in, cover_sem.at[0], cover_sem.at[1], last_source)
+    cover_copy.start()
+    for copy in bulk[1:]:
+        copy.start()
 
     source_units = jnp.zeros((fields, width), jnp.int32)
     for s in range(blocks):
@@ -154,9 +185,6 @@
         for r in range(band):
             source_units += units[:, r * width : (r + 1) * width]
 
-    for load in loads[5:]:
-        load.wait()
-    wetf[...] = wet[...].astype(jnp.float32)
     inverse[...] = wetf[...] / sea[...]
     area_units = jnp.zeros((8, width), jnp.int32)
     for i in range(rows // 8):
@@ -180,20 +208,22 @@
     scaling = jnp.left_shift(jnp.ones_like(power), power).astype(jnp.float32)
     scaling_row = jnp.left_shift(jnp.ones_like(power_row), power_row).astype(jnp.float32)
 
-    low = me * blocks
     slot_of = [jnp.int32(0)] * blocks
-    target_units = jnp.zeros((fields, width), jnp.int32)
-    near_first = sorted(range(n_lon), key=lambda d: min(d, n_lon - d))
-    for d in near_first:
-        if d:
-            route_arrival, bulk_arrival = arrival(d)
-            route_arrival.wait_recv()
-        digits = digits_of(d, low, lambda s, row: row)
+
+    def settle(d, digits):
         for c in range(cap):
             for n in range(blocks):
                 slot_of[n] = jnp.where(digits[c] == n + 1, d * cap + c, slot_of[n])
-        if d:
-            bulk_arrival.wait_recv()
+
+    settle(last_behind, last_digits)
+    target_units = jnp.zeros((fields, width), jnp.int32)
+    for d, source in [(0, me)] + list(zip(behind, sources))[:-1]:
+        if source is not me:
+            route_copy(d, d, source).wait_recv()
+        digits = digits_of(d, low, lambda s, row: row)
+        settle(d, digits)
+        if source is not me:
+            bulk_copy(d, received, d * cap, source).wait_recv()
         for c in range(cap):
             row = jnp.maximum(digits[c] - 1, 0)
             for r in range(band):
@@ -204,6 +234,13 @@
                     units = units * jnp.minimum(digits[c], 1)
                 target_units += units
 
+    cover_copy.wait_recv()
+    for c in range(cap):
+        for r in range(band):
+            cover = cover_in[c * band + r : c * band + r + 1, :]
+            value = outgoing[(n_lon - 2) * cap + c, :, r * width : (r + 1) * width]
+            target_units += (cover * value * quantum).astype(jnp.int32)
+
     mine = jnp.sum(early + placed(row_limbs(target_units), 4), axis=0, keepdims=True)
     sums[pl.ds(0, 1), :] = mine
     sum_copies = []
@@ -215,6 +252,7 @@
         )
         copy.start()
         sum_copies.append(copy)
+    bulk_copy(last_behind, received, last_behind * cap, last_source).wait_recv()
     for n in range(blocks):
         slot = slot_of[n]
         for r in range(band):
@@ -242,7 +280,7 @@
     aligned = pltpu.roll(whole, lanes - 8, 1)
     total_ref[...] = join(whole, aligned) * scaling_row
 
-    for copy in sum_copies + route_copies + bulk:
+    for copy in sum_copies + route_copies + bulk + [cover_copy]:
         copy.wait_send()
 
 
@@ -294,10 +332,12 @@
                 pltpu.SMEM((n_lon, blocks), jnp.int32),
                 pltpu.SMEM((fields,), jnp.int32),
                 pltpu.VMEM((group, lanes), jnp.float32),
+                pltpu.VMEM((cap * cells // width, width), jnp.float32),
+                pltpu.VMEM((cap * cells // width, width), jnp.float32),
                 dma((8,)),
                 dma((n_lon - 1,)), dma((n_lon - 1,)),
                 dma((n_lon - 1,)), dma((n_lon - 1,)),
-                dma((group - 1,)), dma((group - 1,)),
+                dma((group - 1,)), dma((group - 1,)), dma((2,)),
             ],
             compiler_params=pltpu.CompilerParams(collective_id=0, has_side_effects=True),
         )(

time: 18.3 us -> 18.4 us (level)
  no operation moved by 1% of the time
where the time goes in v3:
time: 18.4 us; the launch traced here: 18.2 us
  Pallas kernels  17.6 us (96%)
  between operations  0.64 us (3%)
    pallas_call x1, Pallas kernels, body(): pl.pallas_call(functools.partial(kernel, n_lat, n_lon, cap), out_shape=(p...  16.3 us
    pallas_call x1, Pallas kernels, body(): pl.pallas_call(finish, out_shape=(jax.ShapeDtypeStruct((fields * rows, wi...  1.28 us

profile of v3, /device:TPU:0, one launch (start us, length us, event | category | flops | bytes accessed | tf_op | source)
XLA Modules:
  0.0 18.2 jit_solution(473870579650116099)
XLA Ops:
  0.6 16.3 %shard_map.95 = (f32[512,128]{1,0:T(8,128)S(1)}, f32[64,128]{1,0:T(8,128)S(1)}, f32[2,8,128]{2,1,0:T(8,128)S(1)}, f32[1,128]{1,0:T(1,128)S(1)}) custom-call(f32[16,8,512]{2,1,0:T(8,128)} %bitcast.5, f32[16,512]{1,0:T(8,128)} %bitcast.6, s32[16,512]{1,0:T(8,128)} %bitcast.7, f32[16,512]{1,0:T(8,128)} %bitcast.8, s32[1,16]{1,0:T(1,128)} %route_hbm.1, ...), custom_call_target="tpu_custom_call" | custom-call | tf_op jit(solution)/shard_map/pallas_call | solution.py:312
  16.9 1.3 %shard_map.96 = (f32[512,128]{1,0:T(8,128)}, f32[8]{0:T(128)}) custom-call(f32[512,128]{1,0:T(8,128)S(1)} %get-tuple-element.8.ordered, f32[64,128]{1,0:T(8,128)S(1)} %get-tuple-element.9.wetf, f32[2,8,128]{2,1,0:T(8,128)S(1)} %get-tuple-element.10.coefs, f32[1,128]{1,0:T(1,128)S(1)} %get-tuple-element.11.total_row), custom_call_target="tpu_custom_call" | custom-call | tf_op jit(solution)/shard_map/pallas_call | solution.py:347

commit v4 on v3

--- a/solution.py
+++ b/solution.py
@@ -55,7 +55,7 @@
     n_lat, n_lon, cap,
     flux_hbm, frac_hbm, mask_hbm, area_hbm, route_hbm, sea_hbm, wet_hbm, exp_hbm,
     ordered, wetf, coefs, total_ref,
-    flux, frac, mask, area, sea, wet, inverse, outgoing, received, routes, exps, sums, cover_out, cover_in,
+    flux, frac, mask, area, sea, wet, inverse, outgoing, received, routes, exps, sums, cover_in,
     in_sem, route_send, route_recv, bulk_send, bulk_recv, sum_send, sum_recv, cover_sem,
 ):
     blocks, fields, cells = flux.shape
@@ -146,36 +146,22 @@
         load.wait()
     for step, target in enumerate(steps):
         fill(target, outgoing, step * cap)
+    last_rows = digits_of(0, steps[-1] * blocks, lambda s, row: row)
+    for load in loads[5:]:
+        load.wait()
 
     pl.semaphore_wait(barrier, group - 1)
+    cover_copy = lon_copy(wet, cover_in, cover_sem.at[0], cover_sem.at[1], sources[-1])
     route_copies = [route_copy(d, 0, target) for d, target in zip(away, steps)]
     bulk = [
         bulk_copy(d, outgoing, step * cap, target)
         for step, (d, target) in enumerate(zip(away, steps))
     ]
-    for copy in route_copies + bulk[:1]:
+    for copy in route_copies + [cover_copy] + bulk:
         copy.start()
     fill(me, received, 0)
-
-    for load in loads[5:]:
-        load.wait()
     wetf[...] = wet[...].astype(jnp.float32)
-
     low = me * blocks
-    last_source, last_behind = sources[-1], behind[-1]
-    route_copy(last_behind, last_behind, last_source).wait_recv()
-    last_digits = digits_of(last_behind, low, lambda s, row: row)
-    for c, pick in enumerate(last_digits):
-        row = jnp.maximum(pick - 1, 0)
-        for r in range(band):
-            cover = wetf[pl.ds(row * band + r, 1), :]
-            if not full:
-                cover = cover * jnp.minimum(pick, 1).astype(jnp.float32)
-            cover_out[pl.ds(c * band + r, 1), :] = cover
-    cover_copy = lon_copy(cover_out, cover_in, cover_sem.at[0], cover_sem.at[1], last_source)
-    cover_copy.start()
-    for copy in bulk[1:]:
-        copy.start()
 
     source_units = jnp.zeros((fields, width), jnp.int32)
     for s in range(blocks):
@@ -215,7 +201,6 @@
             for n in range(blocks):
                 slot_of[n] = jnp.where(digits[c] == n + 1, d * cap + c, slot_of[n])
 
-    settle(last_behind, last_digits)
     target_units = jnp.zeros((fields, width), jnp.int32)
     for d, source in [(0, me)] + list(zip(behind, sources))[:-1]:
         if source is not me:
@@ -235,11 +220,15 @@
                 target_units += units
 
     cover_copy.wait_recv()
-    for c in range(cap):
+    for c, pick in enumerate(last_rows):
+        row = jnp.maximum(pick - 1, 0)
         for r in range(band):
-            cover = cover_in[c * band + r : c * band + r + 1, :]
+            cover = cover_in[pl.ds(row * band + r, 1), :].astype(jnp.float32)
             value = outgoing[(n_lon - 2) * cap + c, :, r * width : (r + 1) * width]
-            target_units += (cover * value * quantum).astype(jnp.int32)
+            units = (cover * value * quantum).astype(jnp.int32)
+            if not full:
+                units = units * jnp.minimum(pick, 1)
+            target_units += units
 
     mine = jnp.sum(early + placed(row_limbs(target_units), 4), axis=0, keepdims=True)
     sums[pl.ds(0, 1), :] = mine
@@ -252,7 +241,10 @@
         )
         copy.start()
         sum_copies.append(copy)
-    bulk_copy(last_behind, received, last_behind * cap, last_source).wait_recv()
+    d, source = behind[-1], sources[-1]
+    route_copy(d, d, source).wait_recv()
+    settle(d, digits_of(d, low, lambda s, row: row))
+    bulk_copy(d, received, d * cap, source).wait_recv()
     for n in range(blocks):
         slot = slot_of[n]
         for r in range(band):
@@ -332,8 +324,7 @@
                 pltpu.SMEM((n_lon, blocks), jnp.int32),
                 pltpu.SMEM((fields,), jnp.int32),
                 pltpu.VMEM((group, lanes), jnp.float32),
-                pltpu.VMEM((cap * cells // width, width), jnp.float32),
-                pltpu.VMEM((cap * cells // width, width), jnp.float32),
+                pltpu.VMEM((rows, width), jnp.int32),
                 dma((8,)),
                 dma((n_lon - 1,)), dma((n_lon - 1,)),
                 dma((n_lon - 1,)), dma((n_lon - 1,)),

time: 18.4 us -> 18.9 us (1.027)
  Pallas kernels: 17.6 us -> 18.2 us
    pallas_call x1, Pallas kernels: 16.3 us -> 16.9 us  [body(): pl.pallas_call(functools.partial(kernel, n_lat, n_lon, cap), out_shape=(p...]
where the time goes in v4:
time: 18.9 us; the launch traced here: 18.8 us
  Pallas kernels  18.2 us (96%)
  between operations  0.64 us (3%)
    pallas_call x1, Pallas kernels, body(): pl.pallas_call(functools.partial(kernel, n_lat, n_lon, cap), out_shape=(p...  16.9 us
    pallas_call x1, Pallas kernels, body(): pl.pallas_call(finish, out_shape=(jax.ShapeDtypeStruct((fields * rows, wi...  1.28 us

profile of v4, /device:TPU:0, one launch (start us, length us, event | category | flops | bytes accessed | tf_op | source)
XLA Modules:
  0.0 18.8 jit_solution(3295618415172414084)
XLA Ops:
  0.6 16.9 %shard_map.95 = (f32[512,128]{1,0:T(8,128)S(1)}, f32[64,128]{1,0:T(8,128)S(1)}, f32[2,8,128]{2,1,0:T(8,128)S(1)}, f32[1,128]{1,0:T(1,128)S(1)}) custom-call(f32[16,8,512]{2,1,0:T(8,128)} %bitcast.5, f32[16,512]{1,0:T(8,128)} %bitcast.6, s32[16,512]{1,0:T(8,128)} %bitcast.7, f32[16,512]{1,0:T(8,128)} %bitcast.8, s32[1,16]{1,0:T(1,128)} %route_hbm.1, ...), custom_call_target="tpu_custom_call" | custom-call | tf_op jit(solution)/shard_map/pallas_call | solution.py:304
  17.5 1.3 %shard_map.96 = (f32[512,128]{1,0:T(8,128)}, f32[8]{0:T(128)}) custom-call(f32[512,128]{1,0:T(8,128)S(1)} %get-tuple-element.8.ordered, f32[64,128]{1,0:T(8,128)S(1)} %get-tuple-element.9.wetf, f32[2,8,128]{2,1,0:T(8,128)S(1)} %get-tuple-element.10.coefs, f32[1,128]{1,0:T(1,128)S(1)} %get-tuple-element.11.total_row), custom_call_target="tpu_custom_call" | custom-call | tf_op jit(solution)/shard_map/pallas_call | solution.py:338
